TPU v7x, 32 devices: a whole 2x2x4 slice. The times are simulated.
32 devices in a mesh: lat: 4 (over y, x), lon: 8 (over z, core).
Axes of the slice: x: 2, y: 2, z: 4, core: 2. Of those that a mesh axis runs over, the one named last changes fastest.
Arguments:
- right_side: float32 [8, 768, 1024], P(None, 'lat', 'lon'), may hold values from -16 to 16
- center: float32 [768, 1024], P('lat', 'lon'), may hold values from 3.7 to 5.5
- couplings: float32 [4, 768, 1024], P(None, 'lat', 'lon'), may hold values from 0.15 to 0.45
- land_sea: int32 [768, 1024], P('lat', 'lon'), may hold values 0 or 1
- fold_partner: int32 [1024], replicated, may hold values from 0 to 1023, as said below
Outputs:
- solution: float32 [8, 768, 1024], P(None, 'lat', 'lon')
- residual: float32 [8, 768, 1024], P(None, 'lat', 'lon')
Inputs may be any that keep to these rules, and one draw needn't show every extreme that they name: fold_partner[i] = (s - i) mod 1024 for one integer s, so fold_partner[fold_partner[i]] = i.
All inputs are finite; a program needn't handle non-finite values. No bound on the sum of `land_sea` on one device may be relied on, other than what follows from the above.
Results may differ from a plain program's by a relative error of at most 0.0003.
Values sent between devices are 32-bit elements; how exact they have to be, the bound alone decides.
A program may use at most 64 MiB of HBM per device.

v0:
```python
import jax
import jax.numpy as jnp
from jax import lax
from jax.sharding import PartitionSpec as P

ITERS = 3


def extended(cells, sides, width, closed):
    for axis, dim in sides:
        count = lax.axis_size(axis)
        ends = count if closed else count - 1
        head = lax.slice_in_dim(cells, 0, width, axis=dim)
        tail = lax.slice_in_dim(cells, cells.shape[dim] - width, cells.shape[dim], axis=dim)
        cells = jnp.concatenate(
            [
                lax.ppermute(tail, axis, [(i, (i + 1) % count) for i in range(ends)]),
                cells,
                lax.ppermute(head, axis, [((i + 1) % count, i) for i in range(ends)]),
            ],
            axis=dim,
        )
    return cells


def body(right_side, center, couplings, land_sea, fold_partner):
    row_count, col_count = center.shape
    lat_last = lax.axis_index("lat") == lax.axis_size("lat") - 1
    lat_first = lax.axis_index("lat") == 0
    first_col = lax.axis_index("lon") * col_count
    partner_local = lax.dynamic_slice_in_dim(fold_partner, first_col, col_count, 0)
    ocean_mask = land_sea.astype(jnp.float32)
    north_top = couplings[1, -1, :]
    whole_north = lax.all_gather(north_top, "lon", axis=0, tiled=True)
    fold_coeff = 0.5 * (north_top + jnp.take(whole_north, partner_local, axis=0))
    row_index = lax.broadcasted_iota(jnp.int32, (row_count, col_count), 0)
    top_rows = jnp.logical_and(lat_last, row_index == row_count - 1)
    east_coeff = couplings[0]
    north_coeff = jnp.where(top_rows, fold_coeff[None, :], couplings[1])
    northeast = jnp.where(top_rows, 0.0, couplings[2])
    northwest = jnp.where(top_rows, 0.0, couplings[3])
    stacked = jnp.stack([east_coeff, north_coeff, northeast, northwest])
    coeff_padded = extended(stacked, (("lat", 1), ("lon", 2)), 1, True)
    ghost_rows = lax.broadcasted_iota(jnp.int32, (1, row_count + 2, col_count + 2), 1)
    coeff_padded = jnp.where(jnp.logical_and(lat_first, ghost_rows == 0), 0.0, coeff_padded)
    west_coeff = coeff_padded[0, 1:-1, :-2]
    south_coeff = coeff_padded[1, :-2, 1:-1]
    southwest = coeff_padded[2, :-2, :-2]
    southeast = coeff_padded[3, :-2, 2:]

    def operate(vector):
        top_row = vector[:, -1, :]
        whole_top = lax.all_gather(top_row, "lon", axis=1, tiled=True)
        fold_ghost = jnp.take(whole_top, partner_local, axis=1)
        lon_padded = extended(vector, (("lon", 2),), 1, True)
        padded = extended(lon_padded, (("lat", 1),), 1, False)
        north_row = jnp.where(lat_last, fold_ghost, padded[:, -1, 1:-1])
        padded = padded.at[:, -1, 1:-1].set(north_row)
        upper = padded[:, 2:, 1:-1]
        lower = padded[:, :-2, 1:-1]
        beside = east_coeff * padded[:, 1:-1, 2:] + west_coeff * padded[:, 1:-1, :-2]
        beside = beside + north_coeff * upper + south_coeff * lower
        beside = beside + northeast * padded[:, 2:, 2:] + southwest * padded[:, :-2, :-2]
        beside = beside + northwest * padded[:, 2:, :-2] + southeast * padded[:, :-2, 2:]
        return ocean_mask * (center * vector - beside)

    def paired_sums(residual, scaled, image):
        return lax.psum(
            (jnp.sum(residual * scaled, axis=(1, 2)), jnp.sum(scaled * image, axis=(1, 2))),
            ("lat", "lon"),
        )

    residual = right_side * ocean_mask
    solution = jnp.zeros_like(residual)
    scaled = residual / center
    image = operate(scaled)
    gamma_now, curve = paired_sums(residual, scaled, image)
    step_size = gamma_now / curve
    direction = scaled
    along_dir = image
    for iteration in range(ITERS):
        solution = solution + step_size[:, None, None] * direction
        residual = residual - step_size[:, None, None] * along_dir
        if iteration + 1 < ITERS:
            scaled = residual / center
            image = operate(scaled)
            gamma_next, curve = paired_sums(residual, scaled, image)
            beta_ratio = gamma_next / gamma_now
            step_size = gamma_next / (curve - beta_ratio * gamma_next / step_size)
            direction = scaled + beta_ratio[:, None, None] * direction
            along_dir = image + beta_ratio[:, None, None] * along_dir
            gamma_now = gamma_next
    return (solution, residual)


def solution(mesh):
    return jax.shard_map(
        body,
        mesh=mesh,
        in_specs=(
            P(None, "lat", "lon"),
            P("lat", "lon"),
            P(None, "lat", "lon"),
            P("lat", "lon"),
            P(),
        ),
        out_specs=(P(None, "lat", "lon"), P(None, "lat", "lon")),
        check_vma=False,
    )
```

profile of v0, /device:TPU:0, one launch (start us, length us, event | category | flops | bytes accessed | tf_op | source)
XLA Modules:
  0.0 254.5 jit_solution(16460176406055515500)
XLA Ops:
  0.7 0.8 slice.247
  1.4 13.4 %all-gather.1 = f32[1,1,1024]{2,1,0:T(1,128)S(1)} all-gather(f32[1,1,128]{2,1,0:T(1,128)S(1)} %slice.247), channel_id=3, replica_groups=mesh['lat'=4,'lon'=8] {'lon'}, dimensions={2}, use_global_device_ids=true | all-gather | bytes 4608 | tf_op jit(solution)/shard_map/all_gather | solution.py:34
  14.9 0.8 compare_and_fusion
  15.7 1.0 gather_fusion
  16.6 0.7 fusion.30
  17.3 1.7 slice_select_fusion.2
  19.0 1.5 collective-permute-start.4
  20.6 1.4 collective-permute-start.5
  22.1 1.1 fusion.37
  23.3 1.5 copy.91
  24.8 0.3 copy.90
  25.1 0.5 collective-permute-start
  25.7 1.0 fusion.38
  26.7 1.0 collective-permute-start.6
  27.7 2.5 collective-permute-start.7
  30.2 13.8 %all-gather = f32[8,1,1024]{2,1,0:T(1,128)S(1)} all-gather(f32[8,1,128]{2,1,0:T(1,128)S(1)} %slice.304), channel_id=2, replica_groups=mesh['lat'=4,'lon'=8] {'lon'}, dimensions={2}, use_global_device_ids=true | all-gather | bytes 36864 | tf_op jit(solution)/shard_map/all_gather | solution.py:53
  44.0 0.5 copy.93
  44.6 0.6 gather_fusion.1
  45.4 2.4 maximum_select_fusion
  47.7 0.4 copy.92
  48.1 0.4 copy.94
  48.5 2.5 collective-permute-start.2
  51.0 1.3 collective-permute-start.3
  52.3 2.0 slice_bitcast_fusion.3
  54.3 2.7 %collective-permute-done.3 = f32[8,1,130]{2,0,1:T(8,128)S(1)} collective-permute-done((f32[8,1,130]{2,0,1:T(8,128)S(1)}, f32[8,1,130]{2,0,1:T(8,128)S(1)}, u32[]{:S(2)}, u32[]{:S(2)}) %collective-permute-start.3) | collective-permute-done | bytes 4192 | tf_op jit(solution)/shard_map/ppermute | solution.py:19
  57.0 0.7 pad_maximum_fusion.2
  57.6 0.5 copy.97
  58.2 1.3 scatter.10
  59.6 2.5 multiply_reduce_fusion.4
  62.1 39.8 %all-reduce.2 = (f32[8]{0:T(128)S(1)}, f32[8]{0:T(128)S(1)}) all-reduce(f32[8]{0:T(128)S(1)} %get-tuple-element.50, f32[8]{0:T(128)S(1)} %get-tuple-element.49), channel_id=1, replica_groups=mesh['lat'=4,'lon'=8] {'lat','lon'}, use_global_device_ids=true, to_apply=%region_1.2 | all-reduce | flops 16 | bytes 128 | tf_op jit(solution)/shard_map/psum | solution.py:68
  101.9 2.0 broadcast_divide_fusion.1
  104.2 0.3 copy.99
  104.6 0.3 copy.100
  104.9 3.5 %collective-permute-start.9 = (f32[8,192,1]{1,0,2:T(8,128)S(1)}, f32[8,192,1]{1,0,2:T(8,128)S(1)}, u32[]{:S(2)}, u32[]{:S(2)}) collective-permute-start(f32[8,192,1]{1,0,2:T(8,128)S(1)} %copy.100), channel_id=1, source_target_pairs={{1,0},{2,1},{3,2},{4,3},{5,4},{6,5},{7,6},{0,7},{9,8},{10,9},{11,1... | collective-permute-start | bytes 18440 | tf_op jit(solution)/shard_map/ppermute | solution.py:19
  108.4 1.0 collective-permute-done.8
  109.4 0.3 copy.101
  109.8 0.3 copy.102
  110.3 1.3 collective-permute-start.11
  111.6 4.8 %collective-permute-start.10 = (f32[8,1,130]{2,0,1:T(8,128)S(1)}, f32[8,1,130]{2,0,1:T(8,128)S(1)}, u32[]{:S(2)}, u32[]{:S(2)}) collective-permute-start(f32[8,1,130]{2,0,1:T(8,128)S(1)} %copy.103), channel_id=1, source_target_pairs={{0,8},{8,16},{16,24},{1,9},{9,17},{17,25},{2,10},{10,18},{18,26},{... | collective-permute-start | bytes 12488 | tf_op jit(solution)/shard_map/ppermute | solution.py:17
  116.4 9.9 %all-gather.2 = f32[8,1,1024]{2,1,0:T(1,128)S(1)} all-gather(f32[8,1,128]{2,1,0:T(1,128)S(1)} %slice.322), channel_id=4, replica_groups=mesh['lat'=4,'lon'=8] {'lon'}, dimensions={2}, use_global_device_ids=true | all-gather | bytes 36864 | tf_op jit(solution)/shard_map/all_gather | solution.py:53
  126.3 1.0 copy.121
  127.3 1.7 gather_fusion.2
  129.1 2.1 pad_maximum_fusion
  131.3 1.3 scatter.11
  132.7 3.4 %multiply_reduce_fusion.2 = (f32[8]{0:T(128)S(1)}, f32[8]{0:T(128)S(1)}, f32[8,192,128]{2,1,0:T(8,128)}) fusion(f32[8,192,128]{2,1,0:T(8,128)} %get-tuple-element.71, f32[192,128]{1,0:T(8,128)} %param.14, f32[8,194,130]{2,1,0:T(8,128)S(1)} %scatter.11, f32[192,128]{1,0:T(8,128)} %get-tuple-element.82, f32[192,128]{1,0:T(8,128)S(1)} %bitcast.51, ...), kind=kLoop, calls=%fused_computation.65 | loop fusion | flops 4521968 | bytes 8847424 | tf_op jit(solution)/shard_map/reduce_sum | solution.py:69
  136.0 39.6 %all-reduce.1 = (f32[8]{0:T(128)S(1)}, f32[8]{0:T(128)S(1)}) all-reduce(f32[8]{0:T(128)S(1)} %get-tuple-element.54, f32[8]{0:T(128)S(1)} %get-tuple-element.53), channel_id=1, replica_groups=mesh['lat'=4,'lon'=8] {'lat','lon'}, use_global_device_ids=true, to_apply=%region_5.7 | all-reduce | flops 16 | bytes 128 | tf_op jit(solution)/shard_map/psum | solution.py:68
  175.6 0.6 fusion.32
  176.2 2.8 %broadcast_divide_fusion = (f32[8,192,128]{2,1,0:T(8,128)S(1)}, f32[8,192,128]{2,1,0:T(8,128)}) fusion(f32[192,128]{1,0:T(8,128)} %param.14, f32[8,192,128]{2,1,0:T(8,128)} %get-tuple-element.71, f32[8,192,128]{2,1,0:T(8,128)} %get-tuple-element.69, f32[8,192,128]{2,1,0:T(8,128)} %copy-done.1, f32[8]{0:T(128)S(1)} %get-tuple-element.68, ...), kind=kLoop, calls=%fused_computation.72 | loop fusion | flops 983040 | bytes 4030528 | tf_op jit(solution)/shard_map/div | solution.py:85
  179.4 0.3 copy.109
  179.7 0.3 copy.110
  180.0 3.5 %collective-permute-start.13 = (f32[8,192,1]{1,0,2:T(8,128)S(1)}, f32[8,192,1]{1,0,2:T(8,128)S(1)}, u32[]{:S(2)}, u32[]{:S(2)}) collective-permute-start(f32[8,192,1]{1,0,2:T(8,128)S(1)} %copy.110), channel_id=1, source_target_pairs={{1,0},{2,1},{3,2},{4,3},{5,4},{6,5},{7,6},{0,7},{9,8},{10,9},{11,1... | collective-permute-start | bytes 18440 | tf_op jit(solution)/shard_map/ppermute | solution.py:19
  183.6 1.0 collective-permute-done.12
  184.6 0.3 copy.111
  185.0 0.3 copy.112
  185.4 1.3 collective-permute-start.15
  186.7 4.8 %collective-permute-start.14 = (f32[8,1,130]{2,0,1:T(8,128)S(1)}, f32[8,1,130]{2,0,1:T(8,128)S(1)}, u32[]{:S(2)}, u32[]{:S(2)}) collective-permute-start(f32[8,1,130]{2,0,1:T(8,128)S(1)} %copy.113), channel_id=1, source_target_pairs={{0,8},{8,16},{16,24},{1,9},{9,17},{17,25},{2,10},{10,18},{18,26},{... | collective-permute-start | bytes 12488 | tf_op jit(solution)/shard_map/ppermute | solution.py:17
  191.5 9.9 %all-gather.3 = f32[8,1,1024]{2,1,0:T(1,128)S(1)} all-gather(f32[8,1,128]{2,1,0:T(1,128)S(1)} %slice.334), channel_id=5, replica_groups=mesh['lat'=4,'lon'=8] {'lon'}, dimensions={2}, use_global_device_ids=true | all-gather | bytes 36864 | tf_op jit(solution)/shard_map/all_gather | solution.py:53
  201.5 1.0 copy.122
  202.5 1.7 gather_fusion.3
  204.3 2.1 pad_maximum_fusion.1
  206.5 1.3 scatter.14
  207.9 3.5 %multiply_reduce_fusion = (f32[8]{0:T(128)S(1)}, f32[8]{0:T(128)S(1)}, f32[8,192,128]{2,1,0:T(8,128)}) fusion(f32[8,192,128]{2,1,0:T(8,128)} %get-tuple-element.65, f32[192,128]{1,0:T(8,128)} %param.14, f32[8,194,130]{2,1,0:T(8,128)S(1)} %scatter.14, f32[192,128]{1,0:T(8,128)} %get-tuple-element.82, f32[192,128]{1,0:T(8,128)S(1)} %bitcast.52, ...), kind=kLoop, calls=%fused_computation.61 | loop fusion | flops 4521968 | bytes 8847424 | tf_op jit(solution)/shard_map/reduce_sum | solution.py:69
  211.3 39.4 %all-reduce = (f32[8]{0:T(128)S(1)}, f32[8]{0:T(128)S(1)}) all-reduce(f32[8]{0:T(128)S(1)} %get-tuple-element.52, f32[8]{0:T(128)S(1)} %get-tuple-element.51), channel_id=1, replica_groups=mesh['lat'=4,'lon'=8] {'lat','lon'}, use_global_device_ids=true, to_apply=%region_9.11 | all-reduce | flops 16 | bytes 128 | tf_op jit(solution)/shard_map/psum | solution.py:68
  250.8 3.7 %multiply_subtract_fusion = (f32[8,192,128]{2,1,0:T(8,128)}, f32[8,192,128]{2,1,0:T(8,128)}) fusion(f32[8,192,128]{2,1,0:T(8,128)} %get-tuple-element.65, f32[8,192,128]{2,1,0:T(8,128)} %get-tuple-element.63, f32[8]{0:T(128)S(1)} %get-tuple-element.62, f32[8]{0:T(128)S(1)} %get-tuple-element.61, f32[8,192,128]{2,1,0:T(8,128)} %get-tuple-element.69, ...), kind=kLoop, calls=%fused_computation.59 | loop fusion | flops 3735552 | bytes 6488224 | tf_op jit(solution)/shard_map/sub | solution.py:83
  (90 shorter events, 2.0 us)
Async XLA Ops:
  0.6 21.4 %copy-start.9 = (s32[192,128]{1,0:T(8,128)S(1)}, s32[192,128]{1,0:T(8,128)}, u32[]{:S(2)}) copy-start(s32[192,128]{1,0:T(8,128)} %param.16) | copy-start | bytes 294916
  0.6 21.4 %copy-start.8 = (f32[192,128]{1,0:T(8,128)S(1)}, f32[192,128]{1,0:T(8,128)}, u32[]{:S(2)}) copy-start(f32[192,128]{1,0:T(8,128)} %param.14) | copy-start | bytes 294916
  0.7 21.4 %copy-start = (f32[8,192,128]{2,1,0:T(8,128)S(1)}, f32[8,192,128]{2,1,0:T(8,128)}, u32[]{:S(2)}) copy-start(f32[8,192,128]{2,1,0:T(8,128)} %param.13) | copy-start | bytes 2359300
  19.0 26.3 %copy-start.7 = (f32[1,192,128]{2,1,0:T(8,128)}, f32[1,192,128]{2,1,0:T(8,128)S(1)}, u32[]{:S(2)}) copy-start(f32[1,192,128]{2,1,0:T(8,128)S(1)} %get-tuple-element.97) | copy-start | bytes 294916
  19.0 6.6 %collective-permute-start.4 = (f32[4,1,128]{2,1,0:T(1,128)S(1)}, f32[4,1,128]{2,1,0:T(1,128)S(1)}, u32[]{:S(2)}, u32[]{:S(2)}) collective-permute-start(f32[4,1,128]{2,1,0:T(1,128)S(1)} %get-tuple-element.99), channel_id=1, source_target_pairs={{0,8},{8,16},{16,24},{24,0},{1,9},{9,17},{17,25},{25,1},{2,10},{10... | collective-permute-start | bytes 6152 | tf_op jit(solution)/shard_map/ppermute | solution.py:17
  20.6 5.0 %collective-permute-start.5 = (f32[4,1,128]{2,1,0:T(1,128)S(1)}, f32[4,1,128]{2,1,0:T(1,128)S(1)}, u32[]{:S(2)}, u32[]{:S(2)}) collective-permute-start(f32[4,1,128]{2,1,0:T(1,128)S(1)} %get-tuple-element.100), channel_id=1, source_target_pairs={{8,0},{16,8},{24,16},{0,24},{9,1},{17,9},{25,17},{1,25},{10,2},{18... | collective-permute-start | bytes 6152 | tf_op jit(solution)/shard_map/ppermute | solution.py:19
  24.7 23.4 %collective-permute-start.1 = (f32[8,192,1]{1,0,2:T(8,128)S(1)}, f32[8,192,1]{1,0,2:T(8,128)S(1)}, u32[]{:S(2)}, u32[]{:S(2)}) collective-permute-start(f32[8,192,1]{1,0,2:T(8,128)S(1)} %copy.91), channel_id=1, source_target_pairs={{1,0},{2,1},{3,2},{4,3},{5,4},{6,5},{7,6},{0,7},{9,8},{10,9},{11,1... | collective-permute-start | bytes 18440 | tf_op jit(solution)/shard_map/ppermute | solution.py:19
  25.1 22.7 %collective-permute-start = (f32[8,192,1]{1,0,2:T(8,128)S(1)}, f32[8,192,1]{1,0,2:T(8,128)S(1)}, u32[]{:S(2)}, u32[]{:S(2)}) collective-permute-start(f32[8,192,1]{1,0,2:T(8,128)S(1)} %copy.90), channel_id=1, source_target_pairs={{0,1},{1,2},{2,3},{3,4},{4,5},{5,6},{6,7},{7,0},{8,9},{9,10},{10,1... | collective-permute-start | bytes 18440 | tf_op jit(solution)/shard_map/ppermute | solution.py:17
  26.7 18.7 %collective-permute-start.6 = (f32[4,194,1]{2,1,0:T(8,128)}, f32[4,194,1]{2,1,0:T(8,128)S(1)}, u32[]{:S(2)}, u32[]{:S(2)}) collective-permute-start(f32[4,194,1]{2,1,0:T(8,128)} %get-tuple-element.93), channel_id=1, source_target_pairs={{0,1},{1,2},{2,3},{3,4},{4,5},{5,6},{6,7},{7,0},{8,9},{9,10},{10,1... | collective-permute-start | bytes 9320 | tf_op jit(solution)/shard_map/ppermute | solution.py:17
  27.7 17.6 %collective-permute-start.7 = (f32[4,194,1]{2,1,0:T(8,128)}, f32[4,194,1]{2,1,0:T(8,128)}, u32[]{:S(2)}, u32[]{:S(2)}) collective-permute-start(f32[4,194,1]{2,1,0:T(8,128)} %get-tuple-element.94), channel_id=1, source_target_pairs={{1,0},{2,1},{3,2},{4,3},{5,4},{6,5},{7,6},{0,7},{9,8},{10,9},{11,1... | collective-permute-start | bytes 9320 | tf_op jit(solution)/shard_map/ppermute | solution.py:19
  48.5 5.8 %collective-permute-start.2 = (f32[8,1,130]{2,0,1:T(8,128)S(1)}, f32[8,1,130]{2,0,1:T(8,128)S(1)}, u32[]{:S(2)}, u32[]{:S(2)}) collective-permute-start(f32[8,1,130]{2,0,1:T(8,128)S(1)} %get-tuple-element.79), channel_id=1, source_target_pairs={{0,8},{8,16},{16,24},{1,9},{9,17},{17,25},{2,10},{10,18},{18,26},{... | collective-permute-start | bytes 12488 | tf_op jit(solution)/shard_map/ppermute | solution.py:17
  51.0 5.9 %collective-permute-start.3 = (f32[8,1,130]{2,0,1:T(8,128)S(1)}, f32[8,1,130]{2,0,1:T(8,128)S(1)}, u32[]{:S(2)}, u32[]{:S(2)}) collective-permute-start(f32[8,1,130]{2,0,1:T(8,128)S(1)} %get-tuple-element.80), channel_id=1, source_target_pairs={{8,0},{16,8},{24,16},{9,1},{17,9},{25,17},{10,2},{18,10},{26,18},{... | collective-permute-start | bytes 12488 | tf_op jit(solution)/shard_map/ppermute | solution.py:19
  62.1 41.8 %copy-start.1 = (f32[8,192,128]{2,1,0:T(8,128)}, f32[8,192,128]{2,1,0:T(8,128)S(1)}, u32[]{:S(2)}) copy-start(f32[8,192,128]{2,1,0:T(8,128)S(1)} %get-tuple-element.72) | copy-start | bytes 2359300
  101.9 2.0 copy-start.17
  101.9 2.0 copy-start.19
  101.9 2.0 copy-start.15
  104.5 4.9 %collective-permute-start.8 = (f32[8,192,1]{1,0,2:T(8,128)S(1)}, f32[8,192,1]{1,0,2:T(8,128)S(1)}, u32[]{:S(2)}, u32[]{:S(2)}) collective-permute-start(f32[8,192,1]{1,0,2:T(8,128)S(1)} %copy.99), channel_id=1, source_target_pairs={{0,1},{1,2},{2,3},{3,4},{4,5},{5,6},{6,7},{7,0},{8,9},{9,10},{10,1... | collective-permute-start | bytes 18440 | tf_op jit(solution)/shard_map/ppermute | solution.py:17
  104.9 4.9 %collective-permute-start.9 = (f32[8,192,1]{1,0,2:T(8,128)S(1)}, f32[8,192,1]{1,0,2:T(8,128)S(1)}, u32[]{:S(2)}, u32[]{:S(2)}) collective-permute-start(f32[8,192,1]{1,0,2:T(8,128)S(1)} %copy.100), channel_id=1, source_target_pairs={{1,0},{2,1},{3,2},{4,3},{5,4},{6,5},{7,6},{0,7},{9,8},{10,9},{11,1... | collective-permute-start | bytes 18440 | tf_op jit(solution)/shard_map/ppermute | solution.py:19
  109.7 17.6 %copy-start.4 = (f32[8,192,1]{2,1,0:T(8,128)}, f32[8,192,1]{2,1,0:T(8,128)S(1)}, u32[]{:S(2)}) copy-start(f32[8,192,1]{2,1,0:T(8,128)S(1)} %copy.101) | copy-start | bytes 18436
  110.1 19.0 %copy-start.6 = (f32[8,192,1]{2,1,0:T(8,128)}, f32[8,192,1]{2,1,0:T(8,128)S(1)}, u32[]{:S(2)}) copy-start(f32[8,192,1]{2,1,0:T(8,128)S(1)} %copy.102) | copy-start | bytes 18436
  110.3 18.8 %collective-permute-start.11 = (f32[8,1,130]{2,0,1:T(8,128)S(1)}, f32[8,1,130]{2,0,1:T(8,128)S(1)}, u32[]{:S(2)}, u32[]{:S(2)}) collective-permute-start(f32[8,1,130]{2,0,1:T(8,128)S(1)} %copy.123), channel_id=1, source_target_pairs={{8,0},{16,8},{24,16},{9,1},{17,9},{25,17},{10,2},{18,10},{26,18},{... | collective-permute-start | bytes 12488 | tf_op jit(solution)/shard_map/ppermute | solution.py:19
  111.6 17.5 %collective-permute-start.10 = (f32[8,1,130]{2,0,1:T(8,128)S(1)}, f32[8,1,130]{2,0,1:T(8,128)S(1)}, u32[]{:S(2)}, u32[]{:S(2)}) collective-permute-start(f32[8,1,130]{2,0,1:T(8,128)S(1)} %copy.103), channel_id=1, source_target_pairs={{0,8},{8,16},{16,24},{1,9},{9,17},{17,25},{2,10},{10,18},{18,26},{... | collective-permute-start | bytes 12488 | tf_op jit(solution)/shard_map/ppermute | solution.py:17
  132.6 43.0 %copy-start.18 = (f32[8]{0:T(128)S(1)}, f32[8]{0:T(128)}, u32[]{:S(2)}) copy-start(f32[8]{0:T(128)} %copy-done.17) | copy-start | bytes 100
  132.7 43.0 %copy-start.20 = (f32[8]{0:T(128)S(1)}, f32[8]{0:T(128)}, u32[]{:S(2)}) copy-start(f32[8]{0:T(128)} %copy-done.19) | copy-start | bytes 100
  175.6 3.4 %copy-start.12 = (f32[8]{0:T(128)}, f32[8]{0:T(128)S(1)}, u32[]{:S(2)}) copy-start(f32[8]{0:T(128)S(1)} %get-tuple-element.57) | copy-start | bytes 100
  176.2 2.8 %copy-start.10 = (f32[8]{0:T(128)}, f32[8]{0:T(128)S(1)}, u32[]{:S(2)}) copy-start(f32[8]{0:T(128)S(1)} %get-tuple-element.68) | copy-start | bytes 100
  179.7 4.9 %collective-permute-start.12 = (f32[8,192,1]{1,0,2:T(8,128)S(1)}, f32[8,192,1]{1,0,2:T(8,128)S(1)}, u32[]{:S(2)}, u32[]{:S(2)}) collective-permute-start(f32[8,192,1]{1,0,2:T(8,128)S(1)} %copy.109), channel_id=1, source_target_pairs={{0,1},{1,2},{2,3},{3,4},{4,5},{5,6},{6,7},{7,0},{8,9},{9,10},{10,1... | collective-permute-start | bytes 18440 | tf_op jit(solution)/shard_map/ppermute | solution.py:17
  180.0 4.9 %collective-permute-start.13 = (f32[8,192,1]{1,0,2:T(8,128)S(1)}, f32[8,192,1]{1,0,2:T(8,128)S(1)}, u32[]{:S(2)}, u32[]{:S(2)}) collective-permute-start(f32[8,192,1]{1,0,2:T(8,128)S(1)} %copy.110), channel_id=1, source_target_pairs={{1,0},{2,1},{3,2},{4,3},{5,4},{6,5},{7,6},{0,7},{9,8},{10,9},{11,1... | collective-permute-start | bytes 18440 | tf_op jit(solution)/shard_map/ppermute | solution.py:19
  184.9 17.6 %copy-start.3 = (f32[8,192,1]{2,1,0:T(8,128)}, f32[8,192,1]{2,1,0:T(8,128)S(1)}, u32[]{:S(2)}) copy-start(f32[8,192,1]{2,1,0:T(8,128)S(1)} %copy.111) | copy-start | bytes 18436
  185.3 19.0 %copy-start.5 = (f32[8,192,1]{2,1,0:T(8,128)}, f32[8,192,1]{2,1,0:T(8,128)S(1)}, u32[]{:S(2)}) copy-start(f32[8,192,1]{2,1,0:T(8,128)S(1)} %copy.112) | copy-start | bytes 18436
  185.4 18.8 %collective-permute-start.15 = (f32[8,1,130]{2,0,1:T(8,128)S(1)}, f32[8,1,130]{2,0,1:T(8,128)S(1)}, u32[]{:S(2)}, u32[]{:S(2)}) collective-permute-start(f32[8,1,130]{2,0,1:T(8,128)S(1)} %copy.124), channel_id=1, source_target_pairs={{8,0},{16,8},{24,16},{9,1},{17,9},{25,17},{10,2},{18,10},{26,18},{... | collective-permute-start | bytes 12488 | tf_op jit(solution)/shard_map/ppermute | solution.py:19
  186.7 17.6 %collective-permute-start.14 = (f32[8,1,130]{2,0,1:T(8,128)S(1)}, f32[8,1,130]{2,0,1:T(8,128)S(1)}, u32[]{:S(2)}, u32[]{:S(2)}) collective-permute-start(f32[8,1,130]{2,0,1:T(8,128)S(1)} %copy.113), channel_id=1, source_target_pairs={{0,8},{8,16},{16,24},{1,9},{9,17},{17,25},{2,10},{10,18},{18,26},{... | collective-permute-start | bytes 12488 | tf_op jit(solution)/shard_map/ppermute | solution.py:17
  207.8 42.9 %copy-start.13 = (f32[8]{0:T(128)S(1)}, f32[8]{0:T(128)}, u32[]{:S(2)}) copy-start(f32[8]{0:T(128)} %copy-done.12) | copy-start | bytes 100
  207.8 42.9 %copy-start.14 = (f32[8]{0:T(128)S(1)}, f32[8]{0:T(128)}, u32[]{:S(2)}) copy-start(f32[8]{0:T(128)} %get-tuple-element.67) | copy-start | bytes 100
  207.8 42.9 %copy-start.2 = (f32[8,192,128]{2,1,0:T(8,128)S(1)}, f32[8,192,128]{2,1,0:T(8,128)}, u32[]{:S(2)}) copy-start(f32[8,192,128]{2,1,0:T(8,128)} %copy-done.1) | copy-start | bytes 2359300
  207.9 42.9 %copy-start.11 = (f32[8]{0:T(128)S(1)}, f32[8]{0:T(128)}, u32[]{:S(2)}) copy-start(f32[8]{0:T(128)} %copy-done.10) | copy-start | bytes 100
  207.9 42.9 %copy-start.16 = (f32[8]{0:T(128)S(1)}, f32[8]{0:T(128)}, u32[]{:S(2)}) copy-start(f32[8]{0:T(128)} %copy-done.15) | copy-start | bytes 100
where the time goes:
time: 255 us; the launch traced here: 254 us
  blocking collectives  166 us (65%)
  starting transfers between devices  30.2 us (12%)
  other arithmetic  29.4 us (12%)
  local copies, waits for them, and re-layouts  23 us (9%)
  waiting for transfers between devices  4.77 us (2%)
    psum x3, blocking collectives, paired_sums(): lax.psum((jnp.sum(residual * scaled, axis=(1, 2)), jnp.sum(scaled * image...  119 us
    all_gather x3, blocking collectives, operate(): whole_top = lax.all_gather(top_row, 'lon', axis=1, tiled=True)  33.6 us
    ppermute x8, starting transfers between devices, extended(): lax.ppermute(tail, axis, [(i, (i + 1) % count) for i in range(ends)])  15.2 us
    ppermute x8, starting transfers between devices, extended(): lax.ppermute(head, axis, [((i + 1) % count, i) for i in range(ends)])  15 us
    all_gather x1, blocking collectives, body(): whole_north = lax.all_gather(north_top, 'lon', axis=0, tiled=True)  13.4 us
    reduce_sum x3, other arithmetic, paired_sums(): jnp.sum(scaled * image, axis=(1, 2))  9.31 us
  transfers between devices with their start and end apart: 16, of which 4 were waited for; matrix products, arithmetic and copies ran while one was open for 7% of the time, Pallas kernels for 0%

commit v1 on v0

--- a/solution.py
+++ b/solution.py
@@ -66,8 +66,11 @@
 
     def paired_sums(residual, scaled, image):
         return lax.psum(
-            (jnp.sum(residual * scaled, axis=(1, 2)), jnp.sum(scaled * image, axis=(1, 2))),
-            ("lat", "lon"),
+            lax.psum(
+                (jnp.sum(residual * scaled, axis=(1, 2)), jnp.sum(scaled * image, axis=(1, 2))),
+                "lon",
+            ),
+            "lat",
         )
 
     residual = right_side * ocean_mask

time: 255 us -> 206 us (0.81)
  blocking collectives: 166 us -> 117 us
    psum x3, blocking collectives: 119 us -> 42.4 us  [paired_sums(): lax.psum((jnp.sum(residual * scaled, axis=(1, 2)), jnp.sum(scaled * image...]
    psum x0 -> x3, blocking collectives: none -> 28.4 us  [paired_sums(): lax.psum(lax.psum((jnp.sum(residual * scaled, axis=(1, 2)), jnp.sum(scale...]
  transfers between devices with their start and end apart: 16 -> 16, of which waited for: 4 -> 5; matrix products, arithmetic and copies ran while one was open for 7% -> 8% of each run, Pallas kernels for 0% -> 0%
where the time goes in v1:
time: 206 us; the launch traced here: 205 us
  blocking collectives  117 us (57%)
  starting transfers between devices  29.7 us (14%)
  other arithmetic  29.4 us (14%)
  local copies, waits for them, and re-layouts  23 us (11%)
  waiting for transfers between devices  4.78 us (2%)
    psum x3, blocking collectives, paired_sums(): lax.psum((jnp.sum(residual * scaled, axis=(1, 2)), jnp.sum(scaled * image...  42.4 us
    all_gather x3, blocking collectives, operate(): whole_top = lax.all_gather(top_row, 'lon', axis=1, tiled=True)  33.1 us
    psum x3, blocking collectives, paired_sums(): lax.psum(lax.psum((jnp.sum(residual * scaled, axis=(1, 2)), jnp.sum(scale...  28.4 us
    ppermute x8, starting transfers between devices, extended(): lax.ppermute(head, axis, [((i + 1) % count, i) for i in range(ends)])  15 us
    ppermute x8, starting transfers between devices, extended(): lax.ppermute(tail, axis, [(i, (i + 1) % count) for i in range(ends)])  14.7 us
    all_gather x1, blocking collectives, body(): whole_north = lax.all_gather(north_top, 'lon', axis=0, tiled=True)  13.4 us
    reduce_sum x3, other arithmetic, paired_sums(): jnp.sum(scaled * image, axis=(1, 2))  9.27 us
    div x3, other arithmetic, body(): scaled = residual / center  4.92 us
  transfers between devices with their start and end apart: 16, of which 5 were waited for; matrix products, arithmetic and copies ran while one was open for 8% of the time, Pallas kernels for 0%

profile of v1, /device:TPU:0, one launch (start us, length us, event | category | flops | bytes accessed | tf_op | source)
XLA Modules:
  0.0 205.3 jit_solution(8067492327026669636)
XLA Ops:
  0.7 0.8 slice.247
  1.4 13.4 %all-gather.1 = f32[1,1,1024]{2,1,0:T(1,128)S(1)} all-gather(f32[1,1,128]{2,1,0:T(1,128)S(1)} %slice.247), channel_id=3, replica_groups=mesh['lat'=4,'lon'=8] {'lon'}, dimensions={2}, use_global_device_ids=true | all-gather | bytes 4608 | tf_op jit(solution)/shard_map/all_gather | solution.py:34
  14.9 0.8 compare_and_fusion
  15.7 1.0 gather_fusion
  16.6 0.7 fusion.30
  17.3 1.7 slice_select_fusion.2
  19.0 1.5 collective-permute-start.4
  20.6 1.4 collective-permute-start.5
  22.1 1.1 fusion.37
  23.2 1.5 copy.91
  24.7 0.3 copy.90
  25.1 0.5 collective-permute-start
  25.7 1.0 fusion.38
  26.7 1.0 collective-permute-start.6
  27.7 2.5 %collective-permute-start.7 = (f32[4,194,1]{2,1,0:T(8,128)}, f32[4,194,1]{2,1,0:T(8,128)}, u32[]{:S(2)}, u32[]{:S(2)}) collective-permute-start(f32[4,194,1]{2,1,0:T(8,128)} %get-tuple-element.100), channel_id=1, source_target_pairs={{1,0},{2,1},{3,2},{4,3},{5,4},{6,5},{7,6},{0,7},{9,8},{10,9},{11,1... | collective-permute-start | bytes 9320 | tf_op jit(solution)/shard_map/ppermute | solution.py:19
  30.2 13.8 %all-gather = f32[8,1,1024]{2,1,0:T(1,128)S(1)} all-gather(f32[8,1,128]{2,1,0:T(1,128)S(1)} %slice.304), channel_id=2, replica_groups=mesh['lat'=4,'lon'=8] {'lon'}, dimensions={2}, use_global_device_ids=true | all-gather | bytes 36864 | tf_op jit(solution)/shard_map/all_gather | solution.py:53
  44.0 0.5 copy.93
  44.6 0.6 gather_fusion.1
  45.4 2.3 %maximum_select_fusion = f32[4,194,130]{2,1,0:T(8,128)} fusion(f32[4,194,1]{2,1,0:T(8,128)} %collective-permute-done.7, f32[4,1,128]{2,1,0:T(1,128)S(1)} %collective-permute-done.5, f32[1,192,128]{2,1,0:T(8,128)S(1)} %get-tuple-element.102, f32[1,192,128]{2,1,0:T(8,128)S(1)} %get-tuple-element.103, f32[1,192,128]{2,1,0:T(8,128)S(1)} %get-tuple-element.101, ...), kind=kLoop, calls=%fused_computation.7 | loop fusion | flops 807040 | bytes 807234 | tf_op jit(solution)/shard_map/jit(_where)/select_n | solution.py:45
  47.7 0.4 copy.92
  48.1 0.4 copy.94
  48.5 2.5 %collective-permute-start.2 = (f32[8,1,130]{2,0,1:T(8,128)S(1)}, f32[8,1,130]{2,0,1:T(8,128)S(1)}, u32[]{:S(2)}, u32[]{:S(2)}) collective-permute-start(f32[8,1,130]{2,0,1:T(8,128)S(1)} %get-tuple-element.85), channel_id=1, source_target_pairs={{0,8},{8,16},{16,24},{1,9},{9,17},{17,25},{2,10},{10,18},{18,26},{... | collective-permute-start | bytes 12488 | tf_op jit(solution)/shard_map/ppermute | solution.py:17
  51.0 1.3 collective-permute-start.3
  52.3 1.9 slice_bitcast_fusion.3
  54.3 2.7 %collective-permute-done.3 = f32[8,1,130]{2,0,1:T(8,128)S(1)} collective-permute-done((f32[8,1,130]{2,0,1:T(8,128)S(1)}, f32[8,1,130]{2,0,1:T(8,128)S(1)}, u32[]{:S(2)}, u32[]{:S(2)}) %collective-permute-start.3) | collective-permute-done | bytes 4192 | tf_op jit(solution)/shard_map/ppermute | solution.py:19
  56.9 0.7 pad_maximum_fusion.2
  57.6 0.5 copy.97
  58.2 1.3 scatter.10
  59.6 2.5 %multiply_reduce_fusion.4 = (f32[8]{0:T(128)S(1)}, f32[8]{0:T(128)S(1)}, f32[8,192,128]{2,1,0:T(8,128)S(1)}) fusion(f32[192,128]{1,0:T(8,128)} %param.14, f32[8,192,128]{2,1,0:T(8,128)S(1)} %copy-done, f32[192,128]{1,0:T(8,128)S(1)} %convert_element_type.3, f32[8,194,130]{2,1,0:T(8,128)S(1)} %scatter.10, f32[192,128]{1,0:T(8,128)} %get-tuple-element.88, ...), kind=kLoop, calls=%fused_computation.68 | loop fusion | flops 4718576 | bytes 8847424 | tf_op jit(solution)/shard_map/reduce_sum | solution.py:70
  62.1 13.6 %all-reduce.2 = (f32[8]{0:T(128)S(1)}, f32[8]{0:T(128)S(1)}) all-reduce(f32[8]{0:T(128)S(1)} %get-tuple-element.50, f32[8]{0:T(128)S(1)} %get-tuple-element.49), channel_id=1, replica_groups=mesh['lat'=4,'lon'=8] {'lon'}, use_global_device_ids=true, to_apply=%region_1.2 | all-reduce | flops 16 | bytes 128 | tf_op jit(solution)/shard_map/psum | solution.py:69
  75.7 10.4 %all-reduce.5 = (f32[8]{0:T(128)S(1)}, f32[8]{0:T(128)S(1)}) all-reduce(f32[8]{0:T(128)S(1)} %get-tuple-element.59, f32[8]{0:T(128)S(1)} %get-tuple-element.60), channel_id=1, replica_groups=mesh['lat'=4,'lon'=8] {'lat'}, use_global_device_ids=true, to_apply=%region_2.3 | all-reduce | flops 16 | bytes 128 | tf_op jit(solution)/shard_map/psum | solution.py:68
  86.1 2.0 broadcast_divide_fusion.1
  88.4 0.3 copy.99
  88.7 0.3 copy.100
  89.1 3.5 %collective-permute-start.9 = (f32[8,192,1]{1,0,2:T(8,128)S(1)}, f32[8,192,1]{1,0,2:T(8,128)S(1)}, u32[]{:S(2)}, u32[]{:S(2)}) collective-permute-start(f32[8,192,1]{1,0,2:T(8,128)S(1)} %copy.100), channel_id=1, source_target_pairs={{1,0},{2,1},{3,2},{4,3},{5,4},{6,5},{7,6},{0,7},{9,8},{10,9},{11,1... | collective-permute-start | bytes 18440 | tf_op jit(solution)/shard_map/ppermute | solution.py:19
  92.6 1.0 collective-permute-done.8
  93.6 0.3 copy.101
  94.5 1.3 collective-permute-start.11
  95.8 4.5 %collective-permute-start.10 = (f32[8,1,130]{2,0,1:T(8,128)S(1)}, f32[8,1,130]{2,0,1:T(8,128)S(1)}, u32[]{:S(2)}, u32[]{:S(2)}) collective-permute-start(f32[8,1,130]{2,0,1:T(8,128)S(1)} %copy.103), channel_id=1, source_target_pairs={{0,8},{8,16},{16,24},{1,9},{9,17},{17,25},{2,10},{10,18},{18,26},{... | collective-permute-start | bytes 12488 | tf_op jit(solution)/shard_map/ppermute | solution.py:17
  100.3 9.7 %all-gather.2 = f32[8,1,1024]{2,1,0:T(1,128)S(1)} all-gather(f32[8,1,128]{2,1,0:T(1,128)S(1)} %slice.322), channel_id=4, replica_groups=mesh['lat'=4,'lon'=8] {'lon'}, dimensions={2}, use_global_device_ids=true | all-gather | bytes 36864 | tf_op jit(solution)/shard_map/all_gather | solution.py:53
  110.0 1.0 copy.121
  111.0 1.7 gather_fusion.2
  112.8 2.1 %pad_maximum_fusion = f32[8,194,130]{2,1,0:T(8,128)S(1)} fusion(f32[8,1,130]{2,1,0:T(1,128)S(1)} %copy.106, f32[8,192,1]{2,1,0:T(8,128)} %copy-done.6, f32[8,192,128]{2,1,0:T(8,128)S(1)} %get-tuple-element.76, f32[8,192,1]{2,1,0:T(8,128)} %copy-done.4, f32[8,1,130]{2,1,0:T(1,128)S(1)} %copy.105), kind=kLoop, calls=%fused_computation.4 | loop fusion | flops 807040 | bytes 1614080 | tf_op jit(solution)/shard_map/concatenate | solution.py:15
  114.9 1.3 scatter.11
  116.3 3.4 %multiply_reduce_fusion.2 = (f32[8]{0:T(128)S(1)}, f32[8]{0:T(128)S(1)}, f32[8,192,128]{2,1,0:T(8,128)}) fusion(f32[8,192,128]{2,1,0:T(8,128)} %get-tuple-element.77, f32[192,128]{1,0:T(8,128)} %param.14, f32[8,194,130]{2,1,0:T(8,128)S(1)} %scatter.11, f32[192,128]{1,0:T(8,128)} %get-tuple-element.88, f32[192,128]{1,0:T(8,128)S(1)} %bitcast.51, ...), kind=kLoop, calls=%fused_computation.65 | loop fusion | flops 4521968 | bytes 8847424 | tf_op jit(solution)/shard_map/reduce_sum | solution.py:70
  119.7 14.4 %all-reduce.1 = (f32[8]{0:T(128)S(1)}, f32[8]{0:T(128)S(1)}) all-reduce(f32[8]{0:T(128)S(1)} %get-tuple-element.54, f32[8]{0:T(128)S(1)} %get-tuple-element.53), channel_id=1, replica_groups=mesh['lat'=4,'lon'=8] {'lon'}, use_global_device_ids=true, to_apply=%region_7.9 | all-reduce | flops 16 | bytes 128 | tf_op jit(solution)/shard_map/psum | solution.py:69
  134.1 8.5 %all-reduce.4 = (f32[8]{0:T(128)S(1)}, f32[8]{0:T(128)S(1)}) all-reduce(f32[8]{0:T(128)S(1)} %get-tuple-element.57, f32[8]{0:T(128)S(1)} %get-tuple-element.58), channel_id=1, replica_groups=mesh['lat'=4,'lon'=8] {'lat'}, use_global_device_ids=true, to_apply=%region_8.10 | all-reduce | flops 16 | bytes 128 | tf_op jit(solution)/shard_map/psum | solution.py:68
  142.6 0.6 fusion.32
  143.2 2.9 %broadcast_divide_fusion = (f32[8,192,128]{2,1,0:T(8,128)S(1)}, f32[8,192,128]{2,1,0:T(8,128)}) fusion(f32[192,128]{1,0:T(8,128)} %param.14, f32[8,192,128]{2,1,0:T(8,128)} %get-tuple-element.77, f32[8,192,128]{2,1,0:T(8,128)} %get-tuple-element.75, f32[8,192,128]{2,1,0:T(8,128)} %copy-done.1, f32[8]{0:T(128)S(1)} %get-tuple-element.74, ...), kind=kLoop, calls=%fused_computation.72 | loop fusion | flops 983040 | bytes 4030528 | tf_op jit(solution)/shard_map/div | solution.py:88
  146.3 0.3 copy.109
  146.7 0.3 copy.110
  147.0 3.5 %collective-permute-start.13 = (f32[8,192,1]{1,0,2:T(8,128)S(1)}, f32[8,192,1]{1,0,2:T(8,128)S(1)}, u32[]{:S(2)}, u32[]{:S(2)}) collective-permute-start(f32[8,192,1]{1,0,2:T(8,128)S(1)} %copy.110), channel_id=1, source_target_pairs={{1,0},{2,1},{3,2},{4,3},{5,4},{6,5},{7,6},{0,7},{9,8},{10,9},{11,1... | collective-permute-start | bytes 18440 | tf_op jit(solution)/shard_map/ppermute | solution.py:19
  150.5 1.0 collective-permute-done.12
  152.4 1.3 collective-permute-start.15
  153.7 4.5 %collective-permute-start.14 = (f32[8,1,130]{2,0,1:T(8,128)S(1)}, f32[8,1,130]{2,0,1:T(8,128)S(1)}, u32[]{:S(2)}, u32[]{:S(2)}) collective-permute-start(f32[8,1,130]{2,0,1:T(8,128)S(1)} %copy.113), channel_id=1, source_target_pairs={{0,8},{8,16},{16,24},{1,9},{9,17},{17,25},{2,10},{10,18},{18,26},{... | collective-permute-start | bytes 12488 | tf_op jit(solution)/shard_map/ppermute | solution.py:17
  158.2 9.7 %all-gather.3 = f32[8,1,1024]{2,1,0:T(1,128)S(1)} all-gather(f32[8,1,128]{2,1,0:T(1,128)S(1)} %slice.334), channel_id=5, replica_groups=mesh['lat'=4,'lon'=8] {'lon'}, dimensions={2}, use_global_device_ids=true | all-gather | bytes 36864 | tf_op jit(solution)/shard_map/all_gather | solution.py:53
  167.9 1.0 copy.122
  168.9 1.7 gather_fusion.3
  170.7 2.1 %pad_maximum_fusion.1 = f32[8,194,130]{2,1,0:T(8,128)S(1)} fusion(f32[8,1,130]{2,1,0:T(1,128)S(1)} %copy.116, f32[8,192,1]{2,1,0:T(8,128)} %copy-done.5, f32[8,192,128]{2,1,0:T(8,128)S(1)} %get-tuple-element.70, f32[8,192,1]{2,1,0:T(8,128)} %copy-done.3, f32[8,1,130]{2,1,0:T(1,128)S(1)} %copy.115), kind=kLoop, calls=%fused_computation.5 | loop fusion | flops 807040 | bytes 1614080 | tf_op jit(solution)/shard_map/concatenate | solution.py:15
  172.9 1.3 scatter.14
  174.3 3.4 %multiply_reduce_fusion = (f32[8]{0:T(128)S(1)}, f32[8]{0:T(128)S(1)}, f32[8,192,128]{2,1,0:T(8,128)}) fusion(f32[8,192,128]{2,1,0:T(8,128)} %get-tuple-element.71, f32[192,128]{1,0:T(8,128)} %param.14, f32[8,194,130]{2,1,0:T(8,128)S(1)} %scatter.14, f32[192,128]{1,0:T(8,128)} %get-tuple-element.88, f32[192,128]{1,0:T(8,128)S(1)} %bitcast.52, ...), kind=kLoop, calls=%fused_computation.61 | loop fusion | flops 4521968 | bytes 8847424 | tf_op jit(solution)/shard_map/reduce_sum | solution.py:70
  177.7 14.4 %all-reduce = (f32[8]{0:T(128)S(1)}, f32[8]{0:T(128)S(1)}) all-reduce(f32[8]{0:T(128)S(1)} %get-tuple-element.52, f32[8]{0:T(128)S(1)} %get-tuple-element.51), channel_id=1, replica_groups=mesh['lat'=4,'lon'=8] {'lon'}, use_global_device_ids=true, to_apply=%region_13.15 | all-reduce | flops 16 | bytes 128 | tf_op jit(solution)/shard_map/psum | solution.py:69
  192.1 9.5 %all-reduce.3 = (f32[8]{0:T(128)S(1)}, f32[8]{0:T(128)S(1)}) all-reduce(f32[8]{0:T(128)S(1)} %get-tuple-element.55, f32[8]{0:T(128)S(1)} %get-tuple-element.56), channel_id=1, replica_groups=mesh['lat'=4,'lon'=8] {'lat'}, use_global_device_ids=true, to_apply=%region_14.16 | all-reduce | flops 16 | bytes 128 | tf_op jit(solution)/shard_map/psum | solution.py:68
  201.6 3.7 %multiply_subtract_fusion = (f32[8,192,128]{2,1,0:T(8,128)}, f32[8,192,128]{2,1,0:T(8,128)}) fusion(f32[8,192,128]{2,1,0:T(8,128)} %get-tuple-element.71, f32[8,192,128]{2,1,0:T(8,128)} %get-tuple-element.69, f32[8]{0:T(128)S(1)} %get-tuple-element.68, f32[8]{0:T(128)S(1)} %get-tuple-element.67, f32[8,192,128]{2,1,0:T(8,128)} %get-tuple-element.75, ...), kind=kLoop, calls=%fused_computation.59 | loop fusion | flops 3735552 | bytes 6488224 | tf_op jit(solution)/shard_map/sub | solution.py:86
  (93 shorter events, 2.9 us)
Async XLA Ops:
  0.6 21.4 %copy-start.9 = (s32[192,128]{1,0:T(8,128)S(1)}, s32[192,128]{1,0:T(8,128)}, u32[]{:S(2)}) copy-start(s32[192,128]{1,0:T(8,128)} %param.16) | copy-start | bytes 294916
  0.6 21.4 %copy-start.8 = (f32[192,128]{1,0:T(8,128)S(1)}, f32[192,128]{1,0:T(8,128)}, u32[]{:S(2)}) copy-start(f32[192,128]{1,0:T(8,128)} %param.14) | copy-start | bytes 294916
  0.7 21.4 %copy-start = (f32[8,192,128]{2,1,0:T(8,128)S(1)}, f32[8,192,128]{2,1,0:T(8,128)}, u32[]{:S(2)}) copy-start(f32[8,192,128]{2,1,0:T(8,128)} %param.13) | copy-start | bytes 2359300
  19.0 26.3 %copy-start.7 = (f32[1,192,128]{2,1,0:T(8,128)}, f32[1,192,128]{2,1,0:T(8,128)S(1)}, u32[]{:S(2)}) copy-start(f32[1,192,128]{2,1,0:T(8,128)S(1)} %get-tuple-element.103) | copy-start | bytes 294916
  19.0 6.6 %collective-permute-start.4 = (f32[4,1,128]{2,1,0:T(1,128)S(1)}, f32[4,1,128]{2,1,0:T(1,128)S(1)}, u32[]{:S(2)}, u32[]{:S(2)}) collective-permute-start(f32[4,1,128]{2,1,0:T(1,128)S(1)} %get-tuple-element.105), channel_id=1, source_target_pairs={{0,8},{8,16},{16,24},{24,0},{1,9},{9,17},{17,25},{25,1},{2,10},{10... | collective-permute-start | bytes 6152 | tf_op jit(solution)/shard_map/ppermute | solution.py:17
  20.6 5.0 %collective-permute-start.5 = (f32[4,1,128]{2,1,0:T(1,128)S(1)}, f32[4,1,128]{2,1,0:T(1,128)S(1)}, u32[]{:S(2)}, u32[]{:S(2)}) collective-permute-start(f32[4,1,128]{2,1,0:T(1,128)S(1)} %get-tuple-element.106), channel_id=1, source_target_pairs={{8,0},{16,8},{24,16},{0,24},{9,1},{17,9},{25,17},{1,25},{10,2},{18... | collective-permute-start | bytes 6152 | tf_op jit(solution)/shard_map/ppermute | solution.py:19
  24.7 23.4 %collective-permute-start.1 = (f32[8,192,1]{1,0,2:T(8,128)S(1)}, f32[8,192,1]{1,0,2:T(8,128)S(1)}, u32[]{:S(2)}, u32[]{:S(2)}) collective-permute-start(f32[8,192,1]{1,0,2:T(8,128)S(1)} %copy.91), channel_id=1, source_target_pairs={{1,0},{2,1},{3,2},{4,3},{5,4},{6,5},{7,6},{0,7},{9,8},{10,9},{11,1... | collective-permute-start | bytes 18440 | tf_op jit(solution)/shard_map/ppermute | solution.py:19
  25.1 22.6 %collective-permute-start = (f32[8,192,1]{1,0,2:T(8,128)S(1)}, f32[8,192,1]{1,0,2:T(8,128)S(1)}, u32[]{:S(2)}, u32[]{:S(2)}) collective-permute-start(f32[8,192,1]{1,0,2:T(8,128)S(1)} %copy.90), channel_id=1, source_target_pairs={{0,1},{1,2},{2,3},{3,4},{4,5},{5,6},{6,7},{7,0},{8,9},{9,10},{10,1... | collective-permute-start | bytes 18440 | tf_op jit(solution)/shard_map/ppermute | solution.py:17
  26.7 18.7 %collective-permute-start.6 = (f32[4,194,1]{2,1,0:T(8,128)}, f32[4,194,1]{2,1,0:T(8,128)S(1)}, u32[]{:S(2)}, u32[]{:S(2)}) collective-permute-start(f32[4,194,1]{2,1,0:T(8,128)} %get-tuple-element.99), channel_id=1, source_target_pairs={{0,1},{1,2},{2,3},{3,4},{4,5},{5,6},{6,7},{7,0},{8,9},{9,10},{10,1... | collective-permute-start | bytes 9320 | tf_op jit(solution)/shard_map/ppermute | solution.py:17
  27.7 17.6 %collective-permute-start.7 = (f32[4,194,1]{2,1,0:T(8,128)}, f32[4,194,1]{2,1,0:T(8,128)}, u32[]{:S(2)}, u32[]{:S(2)}) collective-permute-start(f32[4,194,1]{2,1,0:T(8,128)} %get-tuple-element.100), channel_id=1, source_target_pairs={{1,0},{2,1},{3,2},{4,3},{5,4},{6,5},{7,6},{0,7},{9,8},{10,9},{11,1... | collective-permute-start | bytes 9320 | tf_op jit(solution)/shard_map/ppermute | solution.py:19
  48.5 5.7 %collective-permute-start.2 = (f32[8,1,130]{2,0,1:T(8,128)S(1)}, f32[8,1,130]{2,0,1:T(8,128)S(1)}, u32[]{:S(2)}, u32[]{:S(2)}) collective-permute-start(f32[8,1,130]{2,0,1:T(8,128)S(1)} %get-tuple-element.85), channel_id=1, source_target_pairs={{0,8},{8,16},{16,24},{1,9},{9,17},{17,25},{2,10},{10,18},{18,26},{... | collective-permute-start | bytes 12488 | tf_op jit(solution)/shard_map/ppermute | solution.py:17
  51.0 5.9 %collective-permute-start.3 = (f32[8,1,130]{2,0,1:T(8,128)S(1)}, f32[8,1,130]{2,0,1:T(8,128)S(1)}, u32[]{:S(2)}, u32[]{:S(2)}) collective-permute-start(f32[8,1,130]{2,0,1:T(8,128)S(1)} %get-tuple-element.86), channel_id=1, source_target_pairs={{8,0},{16,8},{24,16},{9,1},{17,9},{25,17},{10,2},{18,10},{26,18},{... | collective-permute-start | bytes 12488 | tf_op jit(solution)/shard_map/ppermute | solution.py:19
  62.0 26.0 %copy-start.1 = (f32[8,192,128]{2,1,0:T(8,128)}, f32[8,192,128]{2,1,0:T(8,128)S(1)}, u32[]{:S(2)}) copy-start(f32[8,192,128]{2,1,0:T(8,128)S(1)} %get-tuple-element.78) | copy-start | bytes 2359300
  86.1 2.0 copy-start.17
  86.1 2.0 copy-start.19
  86.1 2.0 copy-start.15
  88.7 4.9 %collective-permute-start.8 = (f32[8,192,1]{1,0,2:T(8,128)S(1)}, f32[8,192,1]{1,0,2:T(8,128)S(1)}, u32[]{:S(2)}, u32[]{:S(2)}) collective-permute-start(f32[8,192,1]{1,0,2:T(8,128)S(1)} %copy.99), channel_id=1, source_target_pairs={{0,1},{1,2},{2,3},{3,4},{4,5},{5,6},{6,7},{7,0},{8,9},{9,10},{10,1... | collective-permute-start | bytes 18440 | tf_op jit(solution)/shard_map/ppermute | solution.py:17
  89.1 4.9 %collective-permute-start.9 = (f32[8,192,1]{1,0,2:T(8,128)S(1)}, f32[8,192,1]{1,0,2:T(8,128)S(1)}, u32[]{:S(2)}, u32[]{:S(2)}) collective-permute-start(f32[8,192,1]{1,0,2:T(8,128)S(1)} %copy.100), channel_id=1, source_target_pairs={{1,0},{2,1},{3,2},{4,3},{5,4},{6,5},{7,6},{0,7},{9,8},{10,9},{11,1... | collective-permute-start | bytes 18440 | tf_op jit(solution)/shard_map/ppermute | solution.py:19
  93.9 17.1 %copy-start.4 = (f32[8,192,1]{2,1,0:T(8,128)}, f32[8,192,1]{2,1,0:T(8,128)S(1)}, u32[]{:S(2)}) copy-start(f32[8,192,1]{2,1,0:T(8,128)S(1)} %copy.101) | copy-start | bytes 18436
  94.3 18.5 %copy-start.6 = (f32[8,192,1]{2,1,0:T(8,128)}, f32[8,192,1]{2,1,0:T(8,128)S(1)}, u32[]{:S(2)}) copy-start(f32[8,192,1]{2,1,0:T(8,128)S(1)} %copy.102) | copy-start | bytes 18436
  94.5 18.3 %collective-permute-start.11 = (f32[8,1,130]{2,0,1:T(8,128)S(1)}, f32[8,1,130]{2,0,1:T(8,128)S(1)}, u32[]{:S(2)}, u32[]{:S(2)}) collective-permute-start(f32[8,1,130]{2,0,1:T(8,128)S(1)} %copy.123), channel_id=1, source_target_pairs={{8,0},{16,8},{24,16},{9,1},{17,9},{25,17},{10,2},{18,10},{26,18},{... | collective-permute-start | bytes 12488 | tf_op jit(solution)/shard_map/ppermute | solution.py:19
  95.8 17.0 %collective-permute-start.10 = (f32[8,1,130]{2,0,1:T(8,128)S(1)}, f32[8,1,130]{2,0,1:T(8,128)S(1)}, u32[]{:S(2)}, u32[]{:S(2)}) collective-permute-start(f32[8,1,130]{2,0,1:T(8,128)S(1)} %copy.103), channel_id=1, source_target_pairs={{0,8},{8,16},{16,24},{1,9},{9,17},{17,25},{2,10},{10,18},{18,26},{... | collective-permute-start | bytes 12488 | tf_op jit(solution)/shard_map/ppermute | solution.py:17
  116.3 26.3 %copy-start.18 = (f32[8]{0:T(128)S(1)}, f32[8]{0:T(128)}, u32[]{:S(2)}) copy-start(f32[8]{0:T(128)} %copy-done.17) | copy-start | bytes 100
  116.3 26.3 %copy-start.20 = (f32[8]{0:T(128)S(1)}, f32[8]{0:T(128)}, u32[]{:S(2)}) copy-start(f32[8]{0:T(128)} %copy-done.19) | copy-start | bytes 100
  142.6 3.5 %copy-start.12 = (f32[8]{0:T(128)}, f32[8]{0:T(128)S(1)}, u32[]{:S(2)}) copy-start(f32[8]{0:T(128)S(1)} %get-tuple-element.63) | copy-start | bytes 100
  143.2 2.9 %copy-start.10 = (f32[8]{0:T(128)}, f32[8]{0:T(128)S(1)}, u32[]{:S(2)}) copy-start(f32[8]{0:T(128)S(1)} %get-tuple-element.74) | copy-start | bytes 100
  146.6 4.9 %collective-permute-start.12 = (f32[8,192,1]{1,0,2:T(8,128)S(1)}, f32[8,192,1]{1,0,2:T(8,128)S(1)}, u32[]{:S(2)}, u32[]{:S(2)}) collective-permute-start(f32[8,192,1]{1,0,2:T(8,128)S(1)} %copy.109), channel_id=1, source_target_pairs={{0,1},{1,2},{2,3},{3,4},{4,5},{5,6},{6,7},{7,0},{8,9},{9,10},{10,1... | collective-permute-start | bytes 18440 | tf_op jit(solution)/shard_map/ppermute | solution.py:17
  147.0 4.9 %collective-permute-start.13 = (f32[8,192,1]{1,0,2:T(8,128)S(1)}, f32[8,192,1]{1,0,2:T(8,128)S(1)}, u32[]{:S(2)}, u32[]{:S(2)}) collective-permute-start(f32[8,192,1]{1,0,2:T(8,128)S(1)} %copy.110), channel_id=1, source_target_pairs={{1,0},{2,1},{3,2},{4,3},{5,4},{6,5},{7,6},{0,7},{9,8},{10,9},{11,1... | collective-permute-start | bytes 18440 | tf_op jit(solution)/shard_map/ppermute | solution.py:19
  151.8 17.1 %copy-start.3 = (f32[8,192,1]{2,1,0:T(8,128)}, f32[8,192,1]{2,1,0:T(8,128)S(1)}, u32[]{:S(2)}) copy-start(f32[8,192,1]{2,1,0:T(8,128)S(1)} %copy.111) | copy-start | bytes 18436
  152.2 18.5 %copy-start.5 = (f32[8,192,1]{2,1,0:T(8,128)}, f32[8,192,1]{2,1,0:T(8,128)S(1)}, u32[]{:S(2)}) copy-start(f32[8,192,1]{2,1,0:T(8,128)S(1)} %copy.112) | copy-start | bytes 18436
  152.4 18.3 %collective-permute-start.15 = (f32[8,1,130]{2,0,1:T(8,128)S(1)}, f32[8,1,130]{2,0,1:T(8,128)S(1)}, u32[]{:S(2)}, u32[]{:S(2)}) collective-permute-start(f32[8,1,130]{2,0,1:T(8,128)S(1)} %copy.124), channel_id=1, source_target_pairs={{8,0},{16,8},{24,16},{9,1},{17,9},{25,17},{10,2},{18,10},{26,18},{... | collective-permute-start | bytes 12488 | tf_op jit(solution)/shard_map/ppermute | solution.py:19
  153.7 17.0 %collective-permute-start.14 = (f32[8,1,130]{2,0,1:T(8,128)S(1)}, f32[8,1,130]{2,0,1:T(8,128)S(1)}, u32[]{:S(2)}, u32[]{:S(2)}) collective-permute-start(f32[8,1,130]{2,0,1:T(8,128)S(1)} %copy.113), channel_id=1, source_target_pairs={{0,8},{8,16},{16,24},{1,9},{9,17},{17,25},{2,10},{10,18},{18,26},{... | collective-permute-start | bytes 12488 | tf_op jit(solution)/shard_map/ppermute | solution.py:17
  174.2 27.4 %copy-start.13 = (f32[8]{0:T(128)S(1)}, f32[8]{0:T(128)}, u32[]{:S(2)}) copy-start(f32[8]{0:T(128)} %copy-done.12) | copy-start | bytes 100
  174.2 27.4 %copy-start.14 = (f32[8]{0:T(128)S(1)}, f32[8]{0:T(128)}, u32[]{:S(2)}) copy-start(f32[8]{0:T(128)} %get-tuple-element.73) | copy-start | bytes 100
  174.2 27.4 %copy-start.2 = (f32[8,192,128]{2,1,0:T(8,128)S(1)}, f32[8,192,128]{2,1,0:T(8,128)}, u32[]{:S(2)}) copy-start(f32[8,192,128]{2,1,0:T(8,128)} %copy-done.1) | copy-start | bytes 2359300
  174.2 27.4 %copy-start.11 = (f32[8]{0:T(128)S(1)}, f32[8]{0:T(128)}, u32[]{:S(2)}) copy-start(f32[8]{0:T(128)} %copy-done.10) | copy-start | bytes 100
  174.3 27.4 %copy-start.16 = (f32[8]{0:T(128)S(1)}, f32[8]{0:T(128)}, u32[]{:S(2)}) copy-start(f32[8]{0:T(128)} %copy-done.15) | copy-start | bytes 100
